TPU v7x, 256 devices: a whole 4x4x8 slice. The times are simulated.
256 devices in a mesh: radial: 64 (over x, z, core), phi: 4 (over y).
Axes of the slice: x: 4, y: 4, z: 8, core: 2. Of those that a mesh axis runs over, the one named last changes fastest.
Arguments:
- conserved: float32 [8, 512, 64, 128], P(None, 'radial', 'phi'), may hold values from -2.5 to 7, as said below
- core_mass: float32 [1], replicated, may hold values from 0.2 to 1
Outputs:
- advanced: float32 [8, 512, 64, 128], P(None, 'radial', 'phi')
- enclosed_mass: float32 [512], P('radial')
Inputs may be any that keep to these rules, and one draw needn't show every extreme that they name: conserved[0] (density) lies between 0.4 and 2.5; conserved[4] exceeds (conserved[1]^2 + conserved[2]^2 + conserved[3]^2)/(2 conserved[0]) by at least 0.6; the speeds |conserved[m]/conserved[0]| stay below 1; conserved[5..7] lie between 0 and conserved[0].
All inputs are finite; a program needn't handle non-finite values.
Results may differ from a plain program's by a relative error of at most 0.0003.
Values sent between devices are 32-bit elements; how exact they have to be, the bound alone decides.
No kernel may reach another device: no remote copies, remote signals or barrier semaphores. Data moves between devices by JAX's collectives and lax.ppermute only.
A program may use at most 64 MiB of HBM per device.

v0:
```python
import math

import jax
import jax.numpy as jnp
from jax import lax
from jax.experimental import pallas as pl
from jax.experimental.pallas import tpu as pltpu
from jax.sharding import PartitionSpec as P

ADIABATIC = 4.0 / 3.0
INNER_RADIUS = 1.0
OUTER_RADIUS = 2.0
COURANT = 0.4
GRAVITY_KICK = 0.004
MINIMUM_DENSITY = 0.05
PRESSURE_FLOOR = 0.01
NV = 8
LANES = 128
SUBLANES = 8
UNROLL1 = 2
UNROLL2 = 4
VMEM_LIMIT = 12 * 1024 * 1024


def step_sizes(radial_total, phi_total, theta_total):
    theta_step = math.pi / theta_total
    phi_step = 2.0 * math.pi / phi_total
    polar_width = INNER_RADIUS * math.sin(0.5 * theta_step) * phi_step
    radial_step = min(2.0 * polar_width, (OUTER_RADIUS - INNER_RADIUS) / radial_total)
    timestep = COURANT * min(radial_step, polar_width)
    return (radial_step, theta_step, phi_step, timestep)


def splat(value):
    return jnp.full((SUBLANES, LANES), value, jnp.float32)


def lane_index():
    return lax.broadcasted_iota(jnp.int32, (SUBLANES, LANES), 1)


def sine_of_zones(theta_step):
    return jnp.sin((lane_index().astype(jnp.float32) + 0.5) * theta_step)


def fill_angles(angles, steps):
    _, theta_step, phi_step, _ = steps
    lane = lane_index().astype(jnp.float32)
    sine = sine_of_zones(theta_step)
    angles[0] = jnp.cos((lane + 0.5) * theta_step) / sine
    angles[1] = jnp.sin((lane + 1.0) * theta_step) * (0.5 / (sine * theta_step))
    angles[2] = jnp.sin(lane * theta_step) * (0.5 / (sine * theta_step))
    angles[3] = 0.5 / (sine * phi_step)


def half_slope(below, above):
    return 0.5 * jnp.maximum(jnp.minimum(above, jnp.maximum(below, 0.0)), jnp.minimum(below, 0.0))


def thermo(u):
    density = jnp.maximum(u[0], MINIMUM_DENSITY)
    inverse = 1.0 / density
    kinetic = (0.5 * inverse) * (u[1] * u[1] + u[2] * u[2] + u[3] * u[3])
    pressure = jnp.maximum((ADIABATIC - 1.0) * (u[4] - kinetic), PRESSURE_FLOOR * density)
    return density, inverse, pressure


def side(u, component):
    _, inverse, pressure = thermo(u)
    normal = u[component] * inverse
    square = (ADIABATIC * pressure) * inverse
    return normal, pressure, jnp.abs(normal) + square * lax.rsqrt(square)


def face_flux(left, right, component):
    vl, pl_, al = side(left, component)
    vr, pr, ar = side(right, component)
    signal = jnp.maximum(al, ar)
    toward, away = vl + signal, vr - signal
    out = [left[k] * toward + right[k] * away for k in range(NV)]
    out[component] = out[component] + (pl_ + pr)
    out[4] = out[4] + (pl_ * vl + pr * vr)
    return out


def next_zone(value, edge):
    turned = pltpu.roll(value, SUBLANES - 1, 1)
    return jnp.where(edge, jnp.concatenate([turned[1:], turned[:1]], axis=0), turned)


def previous_zone(value, edge):
    turned = pltpu.roll(value, 1, 1)
    return jnp.where(edge, jnp.concatenate([turned[-1:], turned[:-1]], axis=0), turned)


def rate_rows(x, kept, angles, rows, wide, first_row, steps, unroll, emit):
    radial_step = steps[0]

    def radius_of(index):
        return INNER_RADIUS + (splat(index) + 0.5) * radial_step

    def states(j, below):
        left, right, above = [], [], []
        for k in range(NV):
            centre = x[j, k, :wide]
            difference = x[j + 1, k, :wide] - centre
            slope = half_slope(below[k], difference)
            left.append(centre + slope)
            right.append(centre - slope)
            above.append(difference)
        return left, right, above

    def keep(left, above):
        for k in range(NV):
            kept[0, k] = left[k]
            kept[1, k] = above[k]

    def radial_face(f):
        inner = [kept[0, k] for k in range(NV)]
        left, right, above = states(f + 2, [kept[1, k] for k in range(NV)])
        keep(left, above)
        face = radius_of(jnp.asarray(first_row + f).astype(jnp.float32)) - 0.5 * radial_step
        area = (0.5 / radial_step) * face * face
        return [area * value for value in face_flux(inner, right, 1)]

    left, _, above = states(1, [x[1, k, :wide] - x[0, k, :wide] for k in range(NV)])
    keep(left, above)
    for k, value in enumerate(radial_face(0)):
        kept[2, k] = value

    last = lane_index() == LANES - 1
    sublane = lax.broadcasted_iota(jnp.int32, (SUBLANES, LANES), 0)
    top, bottom = sublane == SUBLANES - 1, sublane == 0

    def row(r, carry):
        inverse_radius = 1.0 / radius_of((first_row + r).astype(jnp.float32))
        radial_scale = inverse_radius * inverse_radius
        u = [x[r + 2, k, :wide] for k in range(NV)]
        upper = radial_face(r + 1)
        rate = [(kept[2, k] - upper[k]) * radial_scale for k in range(NV)]
        for k in range(NV):
            kept[2, k] = upper[k]
        left, right = [], []
        for k in range(NV):
            after = jnp.where(last, u[k], pltpu.roll(u[k], LANES - 1, 2))
            above = after - u[k]
            slope = half_slope(pltpu.roll(above, 1, 2), above)
            left.append(u[k] + slope)
            right.append(after - pltpu.roll(slope, LANES - 1, 2))
        flux = face_flux(left, right, 2)
        upper, lower = angles[1] * inverse_radius, angles[2] * inverse_radius
        for k in range(NV):
            rate[k] = rate[k] - (upper * flux[k] - lower * pltpu.roll(flux[k], 1, 2))
        left, right = [], []
        for k in range(NV):
            zones = x[r + 2, k]
            after = next_zone(zones, top)
            above = after - zones
            slope = half_slope(previous_zone(above, bottom), above)
            left.append(zones + slope)
            right.append(after - next_zone(slope, top))
        flux = face_flux(left, right, 3)
        scale = angles[3] * inverse_radius
        for k in range(NV):
            rate[k] = rate[k] - scale * (flux[k][:wide] - previous_zone(flux[k], bottom)[:wide])
        density, inverse, pressure = thermo(u)
        cotangent = angles[0]
        vr, vt, vp = u[1] * inverse, u[2] * inverse, u[3] * inverse
        azimuth_push = density * vp * vp
        polar_carry = density * vt
        rate[1] = rate[1] + (2.0 * pressure + (polar_carry * vt + azimuth_push)) * inverse_radius
        rate[2] = rate[2] + ((pressure + azimuth_push) * cotangent - polar_carry * vr) * inverse_radius
        rate[3] = rate[3] - density * vp * (vr + vt * cotangent) * inverse_radius
        emit(r, u, rate)
        return carry

    lax.fori_loop(0, rows, row, 0, unroll=unroll)


def fill_ends(x, rows, position, last_position):
    first = (x.shape[0] - rows) // 2
    last = first + rows - 1

    @pl.when(position == 0)
    def _():
        for k in range(NV):
            x[first - 2, k] = x[first, k]
            x[first - 1, k] = x[first, k]

    @pl.when(position == last_position)
    def _():
        for k in range(NV):
            x[last + 1, k] = x[last, k]
            x[last + 2, k] = x[last, k]


def solution(mesh):
    radial_devices, phi_devices = mesh.shape["radial"], mesh.shape["phi"]
    assert phi_devices == 4 and radial_devices % 2 == 0
    chip = [(i, i ^ 1) for i in range(radial_devices)]
    link = [(i, min(max(i + (1 if i % 2 else -1), 0), radial_devices - 1)) for i in range(radial_devices)]
    clockwise = [(i, (i + 1) % phi_devices) for i in range(phi_devices)]
    counter = [(j, i) for i, j in clockwise]
    pair = [(0, 1), (1, 0), (2, 3), (3, 2)]
    pair_across = [(0, 3), (3, 0), (1, 2), (2, 1)]

    def step(conserved, core_mass):
        _, rows, wedge, theta_cells = conserved.shape
        steps = step_sizes(rows * radial_devices, wedge * phi_devices, theta_cells)
        radial_step, theta_step, phi_step, timestep = steps
        strength = GRAVITY_KICK / timestep
        own = wedge // SUBLANES
        assert rows == 8
        tiles, outer = own + 1, rows + 4
        zones = conserved.reshape(NV, rows, own, SUBLANES, theta_cells)
        position = lax.axis_index("radial").astype(jnp.int32).reshape(1)
        smem = pl.BlockSpec(memory_space=pltpu.SMEM)
        vmem = pl.BlockSpec(memory_space=pltpu.VMEM)
        hbm = pl.BlockSpec(memory_space=pl.ANY)
        f32 = jnp.float32
        limit = pltpu.CompilerParams(vmem_limit_bytes=VMEM_LIMIT)
        angle_scratch = pltpu.VMEM((4, SUBLANES, LANES), f32)

        def shape(*sizes):
            return jax.ShapeDtypeStruct(sizes, f32)

        def radius_at(index):
            return INNER_RADIUS + (splat(index) + 0.5) * radial_step

        def whole(value):
            return jnp.sum(value, axis=(0, 1), keepdims=True)

        side_rows = NV * rows * 4

        def pack(where, u, mass, wedge_before, wedge_after, to_chip, to_link):
            upper = 1 - lax.rem(where[0], 2)
            chip_start, link_start = (rows - 4) * upper, (rows - 4) * (1 - upper)
            sine = sine_of_zones(theta_step)
            lane = lane_index()
            tile = jnp.zeros((SUBLANES, LANES), f32)
            for r in range(rows):
                radius = radius_at((where[0] * rows + r).astype(f32))
                total = sum(u[0, r, t] for t in range(1, own)) + u[0, r, 0]
                shell = whole(total * sine) * (radius * radius * (radial_step * theta_step * phi_step))
                tile = jnp.where(lane == r, shell, tile)
            mass[...] = tile
            for k in range(NV):
                for r in range(rows):
                    at = (k * rows + r) * 4
                    wedge_before[at : at + 4] = u[k, r, 0, 0:4]
                    wedge_after[at : at + 4] = u[k, r, own - 1, 4:8]
                for r in range(4):
                    for t in range(own):
                        to_chip[k, r * own + t] = u[k, chip_start + r, t]
                        to_link[k, r * own + t] = u[k, link_start + r, t]

        slab = shape(NV, 4 * own, SUBLANES, LANES)
        corner = shape(NV, 2, SUBLANES, LANES)
        mass, wedge_before, wedge_after, to_chip, to_link = pl.pallas_call(
            pack,
            out_shape=[shape(8, LANES), shape(side_rows, LANES), shape(side_rows, LANES), slab, slab],
            in_specs=[smem, vmem],
            out_specs=[vmem] * 5,
            compiler_params=limit,
            name="pack",
        )(position, zones)

        wedge_low = lax.ppermute(wedge_after, "phi", clockwise)
        wedge_high = lax.ppermute(wedge_before, "phi", counter)
        from_chip = lax.ppermute(to_chip, "radial", chip)
        from_link = lax.ppermute(to_link, "radial", link)
        mass_beside = lax.ppermute(mass, "phi", pair)
        lanes = lax.broadcasted_iota(jnp.int32, (SUBLANES, LANES), 1)
        pair_mass = jnp.where(lanes == rows, core_mass[0], mass + mass_beside)
        rest_mass = lax.ppermute(pair_mass, "phi", pair_across)

        def add_wedges(mass, rest, masses):
            total = jnp.where(lane_index()[0:1] == rows, mass[0:1], mass[0:1] + rest[0:1])
            for peer in range(radial_devices):
                masses[peer] = total

        masses = pl.pallas_call(
            add_wedges,
            out_shape=shape(radial_devices, 1, LANES),
            in_specs=[vmem] * 2,
            out_specs=vmem,
            compiler_params=limit,
            name="add_wedges",
        )(pair_mass, rest_mass)

        everyone = lax.all_to_all(masses, "radial", 0, 0, tiled=True).reshape(radial_devices, LANES)

        def sides(where, low, high, h, to_chip, to_link):
            upper = 1 - lax.rem(where[0], 2)
            chip_start, link_start = (rows - 2) * upper, (rows - 2) * (1 - upper)
            for k in range(NV):
                for r in range(rows):
                    at = (k * rows + r) * 4
                    h[k, r, 0:4] = high[at : at + 4]
                    h[k, r, 4:8] = low[at : at + 4]
                for r in range(2):
                    to_chip[k, r] = h[k, chip_start + r]
                    to_link[k, r] = h[k, link_start + r]

        h, corner_to_chip, corner_to_link = pl.pallas_call(
            sides,
            out_shape=[shape(NV, rows, SUBLANES, LANES), corner, corner],
            in_specs=[smem] + [vmem] * 2,
            out_specs=[vmem] * 3,
            compiler_params=limit,
            name="sides",
        )(position, wedge_low, wedge_high)

        corner_from_chip = lax.ppermute(corner_to_chip, "radial", chip)
        corner_from_link = lax.ppermute(corner_to_link, "radial", link)

        block = 4

        def fill_window(x, outer_side, u, h, slab, corner):
            ours, theirs = block * (1 - outer_side), block * outer_side
            start = (rows - block) * outer_side
            near, far = theirs + 2 * (1 - outer_side), theirs + 2 * outer_side
            for k in range(NV):
                for r in range(block):
                    for t in range(own):
                        x[ours + r, k, t] = u[k, start + r, t]
                        x[theirs + r, k, t] = slab[k, r * own + t]
                    x[ours + r, k, own] = h[k, start + r]
                for r in range(2):
                    x[near + r, k, own] = corner[k, r]
                    x[far + r, k, own] = splat(1.0)

        def update_window(x, kept, angles, first, out, pulled, base):
            def emit(r, state, rate):
                for k in range(NV):
                    out[base + r, k] = state[k] + timestep * rate[k]
                pulled[base + r, 0] = jnp.maximum(state[0], MINIMUM_DENSITY)
                pulled[base + r, 1] = state[1]

            rate_rows(x, kept, angles, block, tiles, first, steps, UNROLL1, emit)

        def middle_rows(where, u, h, out, pulled, x, kept, angles):
            fill_angles(angles, steps)
            for k in range(NV):
                for r in range(rows):
                    for t in range(own):
                        x[r, k, t] = u[k, r, t]
                    x[r, k, own] = h[k, r]
            update_window(x, kept, angles, where[0] * rows + 2, out, pulled, 0)

        def edge_rows(where, outer_side, u, h, slab, corner, out, pulled, x, kept, angles, ends):
            fill_angles(angles, steps)
            fill_window(x, outer_side, u, h, slab, corner)
            if ends:

                @pl.when(where[0] == 0)
                def _():
                    for k in range(NV):
                        x[2, k] = x[4, k]
                        x[3, k] = x[4, k]

                @pl.when(where[0] == radial_devices - 1)
                def _():
                    for k in range(NV):
                        x[4, k] = x[3, k]
                        x[5, k] = x[3, k]

            first = where[0] * rows - 2 + rows * outer_side
            update_window(x, kept, angles, first, out, pulled, block * outer_side)

        def chip_rows(where, u, h, slab, corner, out, pulled, x, kept, angles):
            edge_rows(where, 1 - lax.rem(where[0], 2), u, h, slab, corner, out, pulled, x, kept, angles, False)

        def link_rows(where, u, h, slab, corner, _out, _pulled, out, pulled, x, kept, angles):
            edge_rows(where, lax.rem(where[0], 2), u, h, slab, corner, out, pulled, x, kept, angles, True)

        window = pltpu.VMEM((block + 4, NV, tiles, SUBLANES, LANES), f32)
        kept_scratch = pltpu.VMEM((3, NV, tiles, SUBLANES, LANES), f32)

        def section_shapes(count):
            return [shape(count, NV, tiles, SUBLANES, LANES), shape(count, 2, tiles, SUBLANES, LANES)]

        middle, middle_pulled = pl.pallas_call(
            middle_rows,
            out_shape=section_shapes(block),
            in_specs=[smem] + [vmem] * 2,
            out_specs=[vmem] * 2,
            scratch_shapes=[window, kept_scratch, angle_scratch],
            compiler_params=limit,
            name="middle_rows",
        )(position, zones, h)
        edge_call = dict(
            out_shape=section_shapes(2 * block),
            out_specs=[vmem] * 2,
            scratch_shapes=[window, kept_scratch, angle_scratch],
            compiler_params=limit,
        )
        edges, edges_pulled = pl.pallas_call(
            chip_rows, in_specs=[smem] + [vmem] * 4, name="chip_rows", **edge_call
        )(position, zones, h, from_chip, corner_from_chip)
        edges, edges_pulled = pl.pallas_call(
            link_rows,
            in_specs=[smem] + [vmem] * 6,
            input_output_aliases={5: 0, 6: 1},
            name="link_rows",
            **edge_call,
        )(position, zones, h, from_link, corner_from_link, edges, edges_pulled)

        def second_section(
            where, masses, u, middle, middle_pulled, edges, edges_pulled, out, enclosed,
            x, kept, angles, pulls, done, sent,
        ):
            fill_angles(angles, steps)
            first = where[0] * rows
            device = lax.broadcasted_iota(jnp.int32, (radial_devices, LANES), 0)
            lane = lax.broadcasted_iota(jnp.int32, (radial_devices, LANES), 1)
            zone = device * rows + lane
            shell = jnp.where(lane < rows, masses[...], 0.0)
            core = splat(1.0) * masses[0:1, rows : rows + 1]
            line = jnp.zeros((1, LANES), f32)
            for j in range(outer):
                index = first + (j - 2)
                weight = jnp.where(zone < index, 1.0, jnp.where(zone == index, 0.5, 0.0))
                inside = whole(shell * weight) + core
                radius = radius_at(index.astype(f32))
                pull = (timestep * strength) * inside / (radius * radius)
                pulls[j] = pull
                line = jnp.where(lane[0:1] == j - 2, inside[0:1], line)
                if j < block:
                    part, pulled, at = edges, edges_pulled, j
                elif j < 2 * block:
                    part, pulled, at = middle, middle_pulled, j - block
                else:
                    part, pulled, at = edges, edges_pulled, j - block
                for k in range(NV):
                    if k == 1:
                        x[j, k] = part[at, k] - pull * pulled[at, 0]
                    elif k == 4:
                        x[j, k] = part[at, k] - pull * pulled[at, 1]
                    else:
                        x[j, k] = part[at, k]
            enclosed[...] = line[:, :rows]
            fill_ends(x, rows, where[0], radial_devices - 1)

            def leave(r):
                return pltpu.make_async_copy(done.at[r], out.at[:, r], sent.at[r])

            def emit(r, state, rate):
                pull = pulls[r + 2]
                density = jnp.maximum(state[0], MINIMUM_DENSITY)
                for k in range(NV):
                    change = timestep * rate[k]
                    if k == 1:
                        change = change - pull * density
                    if k == 4:
                        change = change - pull * state[1]
                    done[r, k] = 0.5 * u[k, r] + 0.5 * (state[k] + change)
                leave(r).start()

            rate_rows(x, kept, angles, rows, own, first, steps, UNROLL2, emit)
            for r in range(rows):
                leave(r).wait()

        advanced, enclosed = pl.pallas_call(
            second_section,
            out_shape=[shape(*zones.shape), shape(1, rows)],
            in_specs=[smem] + [vmem] * 6,
            out_specs=[hbm, vmem],
            scratch_shapes=[
                pltpu.VMEM((outer, NV, tiles, SUBLANES, LANES), f32),
                pltpu.VMEM((3, NV, own, SUBLANES, LANES), f32),
                angle_scratch,
                pltpu.VMEM((outer, SUBLANES, LANES), f32),
                pltpu.VMEM((rows, NV, own, SUBLANES, LANES), f32),
                pltpu.SemaphoreType.DMA((rows,)),
            ],
            compiler_params=limit,
            name="second_section",
        )(position, everyone, zones, middle, middle_pulled, edges, edges_pulled)
        return advanced.reshape(conserved.shape), enclosed.reshape(rows)

    in_specs = (P(None, "radial", "phi", None), P())
    out_specs = (P(None, "radial", "phi", None), P("radial"))
    return jax.shard_map(step, mesh=mesh, in_specs=in_specs, out_specs=out_specs, check_vma=False)
```

profile of v0, /device:TPU:1, one launch (start us, length us, event | category | flops | bytes accessed | tf_op | source)
XLA Modules:
  0.0 43.7 jit_solution(17091311959294172729)
XLA Ops:
  0.6 0.0 copy-start
  0.6 1.0 %copy-done = f32[8,8,16,128]{3,2,1,0:T(8,128)S(1)} copy-done((f32[8,8,16,128]{3,2,1,0:T(8,128)S(1)}, f32[8,8,16,128]{3,2,1,0:T(8,128)}, u32[]{:S(2)}) %copy-start) | copy-done | bytes 524312
  1.7 0.0 copy-start.1
  1.7 0.2 pack.1
  1.9 2.2 %collective-permute-start.2 = (f32[256,128]{1,0:T(8,128)S(1)}, f32[256,128]{1,0:T(8,128)S(1)}, u32[]{:S(2)}, u32[]{:S(2)}) collective-permute-start(f32[256,128]{1,0:T(8,128)S(1)} %get-tuple-element.19), channel_id=1, source_target_pairs={{0,1},{1,2},{2,3},{3,0},{4,5},{5,6},{6,7},{7,4},{8,9},{9,10},{10,1... | collective-permute-start | bytes 393224 | tf_op jit(solution)/shard_map/ppermute | solution.py:268
  4.1 1.5 %collective-permute-start.3 = (f32[256,128]{1,0:T(8,128)S(1)}, f32[256,128]{1,0:T(8,128)S(1)}, u32[]{:S(2)}, u32[]{:S(2)}) collective-permute-start(f32[256,128]{1,0:T(8,128)S(1)} %get-tuple-element.20), channel_id=1, source_target_pairs={{1,0},{2,1},{3,2},{0,3},{5,4},{6,5},{7,6},{4,7},{9,8},{10,9},{11,1... | collective-permute-start | bytes 393224 | tf_op jit(solution)/shard_map/ppermute | solution.py:269
  5.6 2.8 %collective-permute-start.6 = (f32[8,8,8,128]{3,2,1,0:T(8,128)S(1)}, f32[8,8,8,128]{3,2,1,0:T(8,128)S(1)}, u32[]{:S(2)}, u32[]{:S(2)}) collective-permute-start(f32[8,8,8,128]{3,2,1,0:T(8,128)S(1)} %get-tuple-element.26), channel_id=1, source_target_pairs={{0,4},{4,0},{8,12},{12,8},{16,20},{20,16},{24,28},{28,24},{32,36},... | collective-permute-start | bytes 786440 | tf_op jit(solution)/shard_map/ppermute | solution.py:270
  8.4 1.9 %collective-permute-start.4 = (f32[8,8,8,128]{3,2,1,0:T(8,128)S(1)}, f32[8,8,8,128]{3,2,1,0:T(8,128)S(1)}, u32[]{:S(2)}, u32[]{:S(2)}) collective-permute-start(f32[8,8,8,128]{3,2,1,0:T(8,128)S(1)} %get-tuple-element.24), channel_id=1, source_target_pairs={{0,0},{4,8},{8,4},{12,16},{16,12},{20,24},{24,20},{28,32},{32,28},... | collective-permute-start | bytes 786440 | tf_op jit(solution)/shard_map/ppermute | solution.py:271
  10.3 0.1 collective-permute-start
  11.1 1.8 %collective-permute-done = f32[8,128]{1,0:T(8,128)S(1)} collective-permute-done((f32[8,128]{1,0:T(8,128)S(1)}, f32[8,128]{1,0:T(8,128)S(1)}, u32[]{:S(2)}, u32[]{:S(2)}) %collective-permute-start) | collective-permute-done | bytes 4128 | tf_op jit(solution)/shard_map/ppermute | solution.py:272
  12.9 1.3 %collective-permute-start.1 = (f32[8,128]{1,0:T(8,128)S(1)}, f32[8,128]{1,0:T(8,128)S(1)}, u32[]{:S(2)}, u32[]{:S(2)}) collective-permute-start(f32[8,128]{1,0:T(8,128)S(1)} %add_select_fusion.mass), channel_id=1, source_target_pairs={{0,3},{3,0},{1,2},{2,1},{4,7},{7,4},{5,6},{6,5},{8,11},{11,8},{9,1... | collective-permute-start | bytes 12296 | tf_op jit(solution)/shard_map/ppermute | solution.py:275
  14.2 0.0 collective-permute-done.2.low
  14.2 0.0 collective-permute-done.3.high
  14.2 0.1 sides.1
  14.3 0.1 collective-permute-start.7
  14.4 4.2 %collective-permute-start.5 = (f32[8,2,8,128]{3,2,1,0:T(8,128)S(1)}, f32[8,2,8,128]{3,2,1,0:T(8,128)S(1)}, u32[]{:S(2)}, u32[]{:S(2)}) collective-permute-start(f32[8,2,8,128]{3,2,1,0:T(8,128)S(1)} %get-tuple-element.25), channel_id=1, source_target_pairs={{0,0},{4,8},{8,4},{12,16},{16,12},{20,24},{24,20},{28,32},{32,28},... | collective-permute-start | bytes 196616 | tf_op jit(solution)/shard_map/ppermute | solution.py:315
  18.6 0.0 collective-permute-done.1.rest
  18.6 0.6 %add_wedges.1 = f32[64,1,128]{2,1,0:T(1,128)} custom-call(f32[8,128]{1,0:T(8,128)S(1)} %add_select_fusion.mass, f32[8,128]{1,0:T(8,128)S(1)} %collective-permute-done.1.rest), custom_call_target="tpu_custom_call" | custom-call | tf_op jit(solution)/shard_map/add_wedges/pallas_call | solution.py:282
  19.2 11.7 %all-to-all-start = ((f32[64,1,128]{2,1,0:T(1,128)}), f32[64,1,128]{2,1,0:T(1,128)S(1)}, u32[]{:S(2)}, u32[]{:S(2)}) async-start(f32[64,1,128]{2,1,0:T(1,128)} %add_wedges.1), calls=%async_computation | async-start | bytes 65536 | tf_op jit(solution)/shard_map/all_to_all | solution.py:291
  31.0 0.0 copy-done.1
  31.0 1.5 %middle_rows.1 = (f32[4,8,3,8,128]{4,3,2,1,0:T(8,128)S(1)}, f32[4,2,3,8,128]{4,3,2,1,0:T(8,128)S(1)}) custom-call(s32[1]{0:T(128)} %bitcast.where, f32[8,8,2,8,128]{4,3,2,1,0:T(8,128)S(1)} %bitcast.8, f32[8,8,8,128]{3,2,1,0:T(8,128)S(1)} %get-tuple-element.21.h), custom_call_target="tpu_custom_call" | custom-call | tf_op jit(solution)/shard_map/middle_rows/pallas_call | solution.py:383
  32.5 0.0 collective-permute-done.7.corner
  32.5 0.0 collective-permute-done.6.slab
  32.5 1.5 %chip_rows.1 = (f32[8,8,3,8,128]{4,3,2,1,0:T(8,128)S(1)}, f32[8,2,3,8,128]{4,3,2,1,0:T(8,128)S(1)}) custom-call(s32[1]{0:T(128)} %bitcast.where, f32[8,8,2,8,128]{4,3,2,1,0:T(8,128)S(1)} %bitcast.9, f32[8,8,8,128]{3,2,1,0:T(8,128)S(1)} %get-tuple-element.21.h, f32[8,8,8,128]{3,2,1,0:T(8,128)S(1)} %collective-permute-done.6.slab, ...), custom_call_target="tpu_custom_call" | custom-call | tf_op jit(solution)/shard_map/chip_rows/pallas_call | solution.py:398
  34.0 0.0 collective-permute-done.5.corner
  34.0 0.0 collective-permute-done.4.slab
  34.0 1.5 %link_rows.1 = (f32[8,8,3,8,128]{4,3,2,1,0:T(8,128)S(1)}, f32[8,2,3,8,128]{4,3,2,1,0:T(8,128)S(1)}) custom-call(s32[1]{0:T(128)} %bitcast.where, f32[8,8,2,8,128]{4,3,2,1,0:T(8,128)S(1)} %bitcast.10, f32[8,8,8,128]{3,2,1,0:T(8,128)S(1)} %get-tuple-element.21.h, ...), custom_call_target="tpu_custom_call", output_to_operand_aliasing={{0}: (5, {}), {1}: (6, {})} | custom-call | tf_op jit(solution)/shard_map/link_rows/pallas_call | solution.py:401
  35.6 4.6 %all-to-all-done = f32[64,1,128]{2,1,0:T(1,128)S(1)} async-done(((f32[64,1,128]{2,1,0:T(1,128)}), f32[64,1,128]{2,1,0:T(1,128)S(1)}, u32[]{:S(2)}, u32[]{:S(2)}) %all-to-all-start) | async-done | bytes 32800 | tf_op jit(solution)/shard_map/all_to_all | solution.py:291
  40.2 3.5 %second_section.1 = (f32[8,8,2,8,128]{4,3,2,1,0:T(8,128)}, f32[1,8]{1,0:T(1,128)}) custom-call(s32[1]{0:T(128)} %bitcast.where, f32[64,128]{1,0:T(8,128)S(1)} %bitcast.12, f32[8,8,2,8,128]{4,3,2,1,0:T(8,128)S(1)} %bitcast.11, f32[4,8,3,8,128]{4,3,2,1,0:T(8,128)S(1)} %get-tuple-element.22.middle, f32[4,2,3,8,128]{4,3,2,1,0:T(8,128)S(1)} %get-tuple-element.23.middle_pulled, ...), custom_call_target="tpu_custom_call" | custom-call | tf_op jit(solution)/shard_map/second_section/pallas_call | solution.py:464
  (2 shorter events, 0.0 us)
Async XLA Ops:
  0.6 1.0 %copy-start = (f32[8,8,16,128]{3,2,1,0:T(8,128)S(1)}, f32[8,8,16,128]{3,2,1,0:T(8,128)}, u32[]{:S(2)}) copy-start(f32[8,8,16,128]{3,2,1,0:T(8,128)} %param.2) | copy-start | bytes 1572868
  1.7 29.3 %copy-start.1 = (f32[8,8,16,128]{3,2,1,0:T(8,128)S(1)}, f32[8,8,16,128]{3,2,1,0:T(8,128)}, u32[]{:S(2)}) copy-start(f32[8,8,16,128]{3,2,1,0:T(8,128)} %param.2) | copy-start | bytes 1572868
  1.9 12.3 %collective-permute-start.2 = (f32[256,128]{1,0:T(8,128)S(1)}, f32[256,128]{1,0:T(8,128)S(1)}, u32[]{:S(2)}, u32[]{:S(2)}) collective-permute-start(f32[256,128]{1,0:T(8,128)S(1)} %get-tuple-element.19), channel_id=1, source_target_pairs={{0,1},{1,2},{2,3},{3,0},{4,5},{5,6},{6,7},{7,4},{8,9},{9,10},{10,1... | collective-permute-start | bytes 393224 | tf_op jit(solution)/shard_map/ppermute | solution.py:268
  4.1 10.1 %collective-permute-start.3 = (f32[256,128]{1,0:T(8,128)S(1)}, f32[256,128]{1,0:T(8,128)S(1)}, u32[]{:S(2)}, u32[]{:S(2)}) collective-permute-start(f32[256,128]{1,0:T(8,128)S(1)} %get-tuple-element.20), channel_id=1, source_target_pairs={{1,0},{2,1},{3,2},{0,3},{5,4},{6,5},{7,6},{4,7},{9,8},{10,9},{11,1... | collective-permute-start | bytes 393224 | tf_op jit(solution)/shard_map/ppermute | solution.py:269
  5.6 26.9 %collective-permute-start.6 = (f32[8,8,8,128]{3,2,1,0:T(8,128)S(1)}, f32[8,8,8,128]{3,2,1,0:T(8,128)S(1)}, u32[]{:S(2)}, u32[]{:S(2)}) collective-permute-start(f32[8,8,8,128]{3,2,1,0:T(8,128)S(1)} %get-tuple-element.26), channel_id=1, source_target_pairs={{0,4},{4,0},{8,12},{12,8},{16,20},{20,16},{24,28},{28,24},{32,36},... | collective-permute-start | bytes 786440 | tf_op jit(solution)/shard_map/ppermute | solution.py:270
  8.4 25.6 %collective-permute-start.4 = (f32[8,8,8,128]{3,2,1,0:T(8,128)S(1)}, f32[8,8,8,128]{3,2,1,0:T(8,128)S(1)}, u32[]{:S(2)}, u32[]{:S(2)}) collective-permute-start(f32[8,8,8,128]{3,2,1,0:T(8,128)S(1)} %get-tuple-element.24), channel_id=1, source_target_pairs={{0,0},{4,8},{8,4},{12,16},{16,12},{20,24},{24,20},{28,32},{32,28},... | collective-permute-start | bytes 786440 | tf_op jit(solution)/shard_map/ppermute | solution.py:271
  10.3 2.5 %collective-permute-start = (f32[8,128]{1,0:T(8,128)S(1)}, f32[8,128]{1,0:T(8,128)S(1)}, u32[]{:S(2)}, u32[]{:S(2)}) collective-permute-start(f32[8,128]{1,0:T(8,128)S(1)} %get-tuple-element.18), channel_id=1, source_target_pairs={{0,1},{1,0},{2,3},{3,2},{4,5},{5,4},{6,7},{7,6},{8,9},{9,8},{10,11... | collective-permute-start | bytes 12296 | tf_op jit(solution)/shard_map/ppermute | solution.py:272
  12.9 5.7 %collective-permute-start.1 = (f32[8,128]{1,0:T(8,128)S(1)}, f32[8,128]{1,0:T(8,128)S(1)}, u32[]{:S(2)}, u32[]{:S(2)}) collective-permute-start(f32[8,128]{1,0:T(8,128)S(1)} %add_select_fusion.mass), channel_id=1, source_target_pairs={{0,3},{3,0},{1,2},{2,1},{4,7},{7,4},{5,6},{6,5},{8,11},{11,8},{9,1... | collective-permute-start | bytes 12296 | tf_op jit(solution)/shard_map/ppermute | solution.py:275
  14.3 18.2 %collective-permute-start.7 = (f32[8,2,8,128]{3,2,1,0:T(8,128)S(1)}, f32[8,2,8,128]{3,2,1,0:T(8,128)S(1)}, u32[]{:S(2)}, u32[]{:S(2)}) collective-permute-start(f32[8,2,8,128]{3,2,1,0:T(8,128)S(1)} %get-tuple-element.27), channel_id=1, source_target_pairs={{0,4},{4,0},{8,12},{12,8},{16,20},{20,16},{24,28},{28,24},{32,36},... | collective-permute-start | bytes 196616 | tf_op jit(solution)/shard_map/ppermute | solution.py:314
  14.4 19.7 %collective-permute-start.5 = (f32[8,2,8,128]{3,2,1,0:T(8,128)S(1)}, f32[8,2,8,128]{3,2,1,0:T(8,128)S(1)}, u32[]{:S(2)}, u32[]{:S(2)}) collective-permute-start(f32[8,2,8,128]{3,2,1,0:T(8,128)S(1)} %get-tuple-element.25), channel_id=1, source_target_pairs={{0,0},{4,8},{8,4},{12,16},{16,12},{20,24},{24,20},{28,32},{32,28},... | collective-permute-start | bytes 196616 | tf_op jit(solution)/shard_map/ppermute | solution.py:315
  19.2 21.0 %all-to-all-start = ((f32[64,1,128]{2,1,0:T(1,128)}), f32[64,1,128]{2,1,0:T(1,128)S(1)}, u32[]{:S(2)}, u32[]{:S(2)}) async-start(f32[64,1,128]{2,1,0:T(1,128)} %add_wedges.1), calls=%async_computation | async-start | bytes 65536 | tf_op jit(solution)/shard_map/all_to_all | solution.py:291
where the time goes:
time: 43.9 us; the launch traced here: 43.7 us
  starting transfers between devices  25.9 us (59%)
  Pallas kernels  8.92 us (20%)
  waiting for transfers between devices  6.43 us (15%)
  between operations  1.42 us (3%)
  local copies, waits for them, and re-layouts  1.04 us (2%)
    all_to_all x1, starting transfers between devices, step(): lax.all_to_all(masses, 'radial', 0, 0, tiled=True)  11.7 us
    all_to_all x1, waiting for transfers between devices, step(): lax.all_to_all(masses, 'radial', 0, 0, tiled=True)  4.63 us
    ppermute x1, starting transfers between devices, step(): corner_from_link = lax.ppermute(corner_to_link, 'radial', link)  4.21 us
    pallas_call x1, Pallas kernels, step(): pl.pallas_call(second_section, out_shape=[shape(*zones.shape), shape(1, r...  3.48 us
    ppermute x1, starting transfers between devices, step(): from_chip = lax.ppermute(to_chip, 'radial', chip)  2.79 us
    ppermute x1, starting transfers between devices, step(): wedge_low = lax.ppermute(wedge_after, 'phi', clockwise)  2.19 us
    ppermute x1, starting transfers between devices, step(): from_link = lax.ppermute(to_link, 'radial', link)  1.91 us
    ppermute x1, waiting for transfers between devices, step(): mass_beside = lax.ppermute(mass, 'phi', pair)  1.79 us
  transfers between devices with their start and end apart: 9, of which 2 were waited for; matrix products, arithmetic and copies ran while one was open for 0% of the time, Pallas kernels for 12%

commit v1 on v0

--- a/solution.py
+++ b/solution.py
@@ -232,7 +232,13 @@
 
         side_rows = NV * rows * 4
 
-        def pack(where, u, mass, wedge_before, wedge_after, to_chip, to_link):
+        def pack(where, far, mass, wedge_before, wedge_after, to_chip, to_link, u, arrived):
+            def fetch(k):
+                return pltpu.make_async_copy(far.at[k], u.at[k], arrived.at[k])
+
+            for k in range(NV):
+                fetch(k).start()
+            fetch(0).wait()
             upper = 1 - lax.rem(where[0], 2)
             chip_start, link_start = (rows - 4) * upper, (rows - 4) * (1 - upper)
             sine = sine_of_zones(theta_step)
@@ -245,6 +251,8 @@
                 tile = jnp.where(lane == r, shell, tile)
             mass[...] = tile
             for k in range(NV):
+                if k:
+                    fetch(k).wait()
                 for r in range(rows):
                     at = (k * rows + r) * 4
                     wedge_before[at : at + 4] = u[k, r, 0, 0:4]
@@ -259,11 +267,15 @@
         mass, wedge_before, wedge_after, to_chip, to_link = pl.pallas_call(
             pack,
             out_shape=[shape(8, LANES), shape(side_rows, LANES), shape(side_rows, LANES), slab, slab],
-            in_specs=[smem, vmem],
+            in_specs=[smem, pl.BlockSpec(memory_space=pltpu.HBM)],
+            scratch_shapes=[
+                pltpu.VMEM((NV, rows, own, SUBLANES, theta_cells), f32),
+                pltpu.SemaphoreType.DMA((NV,)),
+            ],
             out_specs=[vmem] * 5,
             compiler_params=limit,
             name="pack",
-        )(position, zones)
+        )(position, pltpu.with_memory_space_constraint(zones, pltpu.HBM))
 
         wedge_low = lax.ppermute(wedge_after, "phi", clockwise)
         wedge_high = lax.ppermute(wedge_before, "phi", counter)

time: 43.9 us -> 43.9 us (level)
  local copies, waits for them, and re-layouts: 1.04 us -> 0.01 us
  Pallas kernels: 8.92 us -> 9.95 us
    unnamed x4 -> x2, local copies, waits for them, and re-layouts: 1.04 us -> 0.01 us
    pallas_call x1, Pallas kernels: 0.19 us -> 1.23 us  [step(): pl.pallas_call(pack, out_shape=[shape(8, LANES), shape(side_rows, LANES),...]
where the time goes in v1:
time: 43.9 us; the launch traced here: 43.7 us
  starting transfers between devices  25.9 us (59%)
  Pallas kernels  9.95 us (23%)
  waiting for transfers between devices  6.43 us (15%)
  between operations  1.42 us (3%)
    all_to_all x1, starting transfers between devices, step(): lax.all_to_all(masses, 'radial', 0, 0, tiled=True)  11.7 us
    all_to_all x1, waiting for transfers between devices, step(): lax.all_to_all(masses, 'radial', 0, 0, tiled=True)  4.63 us
    ppermute x1, starting transfers between devices, step(): corner_from_link = lax.ppermute(corner_to_link, 'radial', link)  4.21 us
    pallas_call x1, Pallas kernels, step(): pl.pallas_call(second_section, out_shape=[shape(*zones.shape), shape(1, r...  3.48 us
    ppermute x1, starting transfers between devices, step(): from_chip = lax.ppermute(to_chip, 'radial', chip)  2.79 us
    ppermute x1, starting transfers between devices, step(): wedge_low = lax.ppermute(wedge_after, 'phi', clockwise)  2.19 us
    ppermute x1, starting transfers between devices, step(): from_link = lax.ppermute(to_link, 'radial', link)  1.91 us
    ppermute x1, waiting for transfers between devices, step(): mass_beside = lax.ppermute(mass, 'phi', pair)  1.79 us
  transfers between devices with their start and end apart: 9, of which 2 were waited for; matrix products, arithmetic and copies ran while one was open for 0% of the time, Pallas kernels for 12%

profile of v1, /device:TPU:1, one launch (start us, length us, event | category | flops | bytes accessed | tf_op | source)
XLA Modules:
  0.0 43.7 jit_solution(13387288232429936643)
XLA Ops:
  0.6 0.0 copy-start
  0.6 1.2 %pack.1 = (f32[8,128]{1,0:T(8,128)S(1)}, f32[256,128]{1,0:T(8,128)S(1)}, f32[256,128]{1,0:T(8,128)S(1)}, f32[8,8,8,128]{3,2,1,0:T(8,128)S(1)}, f32[8,8,8,128]{3,2,1,0:T(8,128)S(1)}) custom-call(s32[1]{0:T(128)} %bitcast.where, f32[8,8,2,8,128]{4,3,2,1,0:T(8,128)} %bitcast.7), custom_call_target="tpu_custom_call" | custom-call | tf_op jit(solution)/shard_map/pack/pallas_call | solution.py:267
  1.9 2.2 %collective-permute-start.2 = (f32[256,128]{1,0:T(8,128)S(1)}, f32[256,128]{1,0:T(8,128)S(1)}, u32[]{:S(2)}, u32[]{:S(2)}) collective-permute-start(f32[256,128]{1,0:T(8,128)S(1)} %get-tuple-element.19), channel_id=1, source_target_pairs={{0,1},{1,2},{2,3},{3,0},{4,5},{5,6},{6,7},{7,4},{8,9},{9,10},{10,1... | collective-permute-start | bytes 393224 | tf_op jit(solution)/shard_map/ppermute | solution.py:280
  4.1 1.5 %collective-permute-start.3 = (f32[256,128]{1,0:T(8,128)S(1)}, f32[256,128]{1,0:T(8,128)S(1)}, u32[]{:S(2)}, u32[]{:S(2)}) collective-permute-start(f32[256,128]{1,0:T(8,128)S(1)} %get-tuple-element.20), channel_id=1, source_target_pairs={{1,0},{2,1},{3,2},{0,3},{5,4},{6,5},{7,6},{4,7},{9,8},{10,9},{11,1... | collective-permute-start | bytes 393224 | tf_op jit(solution)/shard_map/ppermute | solution.py:281
  5.6 2.8 %collective-permute-start.6 = (f32[8,8,8,128]{3,2,1,0:T(8,128)S(1)}, f32[8,8,8,128]{3,2,1,0:T(8,128)S(1)}, u32[]{:S(2)}, u32[]{:S(2)}) collective-permute-start(f32[8,8,8,128]{3,2,1,0:T(8,128)S(1)} %get-tuple-element.26), channel_id=1, source_target_pairs={{0,4},{4,0},{8,12},{12,8},{16,20},{20,16},{24,28},{28,24},{32,36},... | collective-permute-start | bytes 786440 | tf_op jit(solution)/shard_map/ppermute | solution.py:282
  8.4 1.9 %collective-permute-start.4 = (f32[8,8,8,128]{3,2,1,0:T(8,128)S(1)}, f32[8,8,8,128]{3,2,1,0:T(8,128)S(1)}, u32[]{:S(2)}, u32[]{:S(2)}) collective-permute-start(f32[8,8,8,128]{3,2,1,0:T(8,128)S(1)} %get-tuple-element.24), channel_id=1, source_target_pairs={{0,0},{4,8},{8,4},{12,16},{16,12},{20,24},{24,20},{28,32},{32,28},... | collective-permute-start | bytes 786440 | tf_op jit(solution)/shard_map/ppermute | solution.py:283
  10.3 0.1 collective-permute-start
  11.1 1.8 %collective-permute-done = f32[8,128]{1,0:T(8,128)S(1)} collective-permute-done((f32[8,128]{1,0:T(8,128)S(1)}, f32[8,128]{1,0:T(8,128)S(1)}, u32[]{:S(2)}, u32[]{:S(2)}) %collective-permute-start) | collective-permute-done | bytes 4128 | tf_op jit(solution)/shard_map/ppermute | solution.py:284
  12.9 1.3 %collective-permute-start.1 = (f32[8,128]{1,0:T(8,128)S(1)}, f32[8,128]{1,0:T(8,128)S(1)}, u32[]{:S(2)}, u32[]{:S(2)}) collective-permute-start(f32[8,128]{1,0:T(8,128)S(1)} %add_select_fusion.mass), channel_id=1, source_target_pairs={{0,3},{3,0},{1,2},{2,1},{4,7},{7,4},{5,6},{6,5},{8,11},{11,8},{9,1... | collective-permute-start | bytes 12296 | tf_op jit(solution)/shard_map/ppermute | solution.py:287
  14.2 0.0 collective-permute-done.2.low
  14.2 0.0 collective-permute-done.3.high
  14.2 0.1 sides.1
  14.3 0.1 collective-permute-start.7
  14.4 4.2 %collective-permute-start.5 = (f32[8,2,8,128]{3,2,1,0:T(8,128)S(1)}, f32[8,2,8,128]{3,2,1,0:T(8,128)S(1)}, u32[]{:S(2)}, u32[]{:S(2)}) collective-permute-start(f32[8,2,8,128]{3,2,1,0:T(8,128)S(1)} %get-tuple-element.25), channel_id=1, source_target_pairs={{0,0},{4,8},{8,4},{12,16},{16,12},{20,24},{24,20},{28,32},{32,28},... | collective-permute-start | bytes 196616 | tf_op jit(solution)/shard_map/ppermute | solution.py:327
  18.6 0.0 collective-permute-done.1.rest
  18.6 0.6 %add_wedges.1 = f32[64,1,128]{2,1,0:T(1,128)} custom-call(f32[8,128]{1,0:T(8,128)S(1)} %add_select_fusion.mass, f32[8,128]{1,0:T(8,128)S(1)} %collective-permute-done.1.rest), custom_call_target="tpu_custom_call" | custom-call | tf_op jit(solution)/shard_map/add_wedges/pallas_call | solution.py:294
  19.2 11.7 %all-to-all-start = ((f32[64,1,128]{2,1,0:T(1,128)}), f32[64,1,128]{2,1,0:T(1,128)S(1)}, u32[]{:S(2)}, u32[]{:S(2)}) async-start(f32[64,1,128]{2,1,0:T(1,128)} %add_wedges.1), calls=%async_computation | async-start | bytes 65536 | tf_op jit(solution)/shard_map/all_to_all | solution.py:303
  31.0 0.0 copy-done
  31.0 1.5 %middle_rows.1 = (f32[4,8,3,8,128]{4,3,2,1,0:T(8,128)S(1)}, f32[4,2,3,8,128]{4,3,2,1,0:T(8,128)S(1)}) custom-call(s32[1]{0:T(128)} %bitcast.where, f32[8,8,2,8,128]{4,3,2,1,0:T(8,128)S(1)} %bitcast.8, f32[8,8,8,128]{3,2,1,0:T(8,128)S(1)} %get-tuple-element.21.h), custom_call_target="tpu_custom_call" | custom-call | tf_op jit(solution)/shard_map/middle_rows/pallas_call | solution.py:395
  32.5 0.0 collective-permute-done.7.corner
  32.5 0.0 collective-permute-done.6.slab
  32.5 1.5 %chip_rows.1 = (f32[8,8,3,8,128]{4,3,2,1,0:T(8,128)S(1)}, f32[8,2,3,8,128]{4,3,2,1,0:T(8,128)S(1)}) custom-call(s32[1]{0:T(128)} %bitcast.where, f32[8,8,2,8,128]{4,3,2,1,0:T(8,128)S(1)} %bitcast.9, f32[8,8,8,128]{3,2,1,0:T(8,128)S(1)} %get-tuple-element.21.h, f32[8,8,8,128]{3,2,1,0:T(8,128)S(1)} %collective-permute-done.6.slab, ...), custom_call_target="tpu_custom_call" | custom-call | tf_op jit(solution)/shard_map/chip_rows/pallas_call | solution.py:410
  34.0 0.0 collective-permute-done.5.corner
  34.0 0.0 collective-permute-done.4.slab
  34.0 1.5 %link_rows.1 = (f32[8,8,3,8,128]{4,3,2,1,0:T(8,128)S(1)}, f32[8,2,3,8,128]{4,3,2,1,0:T(8,128)S(1)}) custom-call(s32[1]{0:T(128)} %bitcast.where, f32[8,8,2,8,128]{4,3,2,1,0:T(8,128)S(1)} %bitcast.10, f32[8,8,8,128]{3,2,1,0:T(8,128)S(1)} %get-tuple-element.21.h, ...), custom_call_target="tpu_custom_call", output_to_operand_aliasing={{0}: (5, {}), {1}: (6, {})} | custom-call | tf_op jit(solution)/shard_map/link_rows/pallas_call | solution.py:413
  35.6 4.6 %all-to-all-done = f32[64,1,128]{2,1,0:T(1,128)S(1)} async-done(((f32[64,1,128]{2,1,0:T(1,128)}), f32[64,1,128]{2,1,0:T(1,128)S(1)}, u32[]{:S(2)}, u32[]{:S(2)}) %all-to-all-start) | async-done | bytes 32800 | tf_op jit(solution)/shard_map/all_to_all | solution.py:303
  40.2 3.5 %second_section.1 = (f32[8,8,2,8,128]{4,3,2,1,0:T(8,128)}, f32[1,8]{1,0:T(1,128)}) custom-call(s32[1]{0:T(128)} %bitcast.where, f32[64,128]{1,0:T(8,128)S(1)} %bitcast.12, f32[8,8,2,8,128]{4,3,2,1,0:T(8,128)S(1)} %bitcast.11, f32[4,8,3,8,128]{4,3,2,1,0:T(8,128)S(1)} %get-tuple-element.22.middle, f32[4,2,3,8,128]{4,3,2,1,0:T(8,128)S(1)} %get-tuple-element.23.middle_pulled, ...), custom_call_target="tpu_custom_call" | custom-call | tf_op jit(solution)/shard_map/second_section/pallas_call | solution.py:476
  (2 shorter events, 0.0 us)
Async XLA Ops:
  0.6 30.3 %copy-start = (f32[8,8,16,128]{3,2,1,0:T(8,128)S(1)}, f32[8,8,16,128]{3,2,1,0:T(8,128)}, u32[]{:S(2)}) copy-start(f32[8,8,16,128]{3,2,1,0:T(8,128)} %param.2) | copy-start | bytes 1572868
  1.9 12.3 %collective-permute-start.2 = (f32[256,128]{1,0:T(8,128)S(1)}, f32[256,128]{1,0:T(8,128)S(1)}, u32[]{:S(2)}, u32[]{:S(2)}) collective-permute-start(f32[256,128]{1,0:T(8,128)S(1)} %get-tuple-element.19), channel_id=1, source_target_pairs={{0,1},{1,2},{2,3},{3,0},{4,5},{5,6},{6,7},{7,4},{8,9},{9,10},{10,1... | collective-permute-start | bytes 393224 | tf_op jit(solution)/shard_map/ppermute | solution.py:280
  4.1 10.1 %collective-permute-start.3 = (f32[256,128]{1,0:T(8,128)S(1)}, f32[256,128]{1,0:T(8,128)S(1)}, u32[]{:S(2)}, u32[]{:S(2)}) collective-permute-start(f32[256,128]{1,0:T(8,128)S(1)} %get-tuple-element.20), channel_id=1, source_target_pairs={{1,0},{2,1},{3,2},{0,3},{5,4},{6,5},{7,6},{4,7},{9,8},{10,9},{11,1... | collective-permute-start | bytes 393224 | tf_op jit(solution)/shard_map/ppermute | solution.py:281
  5.6 26.9 %collective-permute-start.6 = (f32[8,8,8,128]{3,2,1,0:T(8,128)S(1)}, f32[8,8,8,128]{3,2,1,0:T(8,128)S(1)}, u32[]{:S(2)}, u32[]{:S(2)}) collective-permute-start(f32[8,8,8,128]{3,2,1,0:T(8,128)S(1)} %get-tuple-element.26), channel_id=1, source_target_pairs={{0,4},{4,0},{8,12},{12,8},{16,20},{20,16},{24,28},{28,24},{32,36},... | collective-permute-start | bytes 786440 | tf_op jit(solution)/shard_map/ppermute | solution.py:282
  8.4 25.6 %collective-permute-start.4 = (f32[8,8,8,128]{3,2,1,0:T(8,128)S(1)}, f32[8,8,8,128]{3,2,1,0:T(8,128)S(1)}, u32[]{:S(2)}, u32[]{:S(2)}) collective-permute-start(f32[8,8,8,128]{3,2,1,0:T(8,128)S(1)} %get-tuple-element.24), channel_id=1, source_target_pairs={{0,0},{4,8},{8,4},{12,16},{16,12},{20,24},{24,20},{28,32},{32,28},... | collective-permute-start | bytes 786440 | tf_op jit(solution)/shard_map/ppermute | solution.py:283
  10.3 2.5 %collective-permute-start = (f32[8,128]{1,0:T(8,128)S(1)}, f32[8,128]{1,0:T(8,128)S(1)}, u32[]{:S(2)}, u32[]{:S(2)}) collective-permute-start(f32[8,128]{1,0:T(8,128)S(1)} %get-tuple-element.18), channel_id=1, source_target_pairs={{0,1},{1,0},{2,3},{3,2},{4,5},{5,4},{6,7},{7,6},{8,9},{9,8},{10,11... | collective-permute-start | bytes 12296 | tf_op jit(solution)/shard_map/ppermute | solution.py:284
  12.9 5.7 %collective-permute-start.1 = (f32[8,128]{1,0:T(8,128)S(1)}, f32[8,128]{1,0:T(8,128)S(1)}, u32[]{:S(2)}, u32[]{:S(2)}) collective-permute-start(f32[8,128]{1,0:T(8,128)S(1)} %add_select_fusion.mass), channel_id=1, source_target_pairs={{0,3},{3,0},{1,2},{2,1},{4,7},{7,4},{5,6},{6,5},{8,11},{11,8},{9,1... | collective-permute-start | bytes 12296 | tf_op jit(solution)/shard_map/ppermute | solution.py:287
  14.3 18.2 %collective-permute-start.7 = (f32[8,2,8,128]{3,2,1,0:T(8,128)S(1)}, f32[8,2,8,128]{3,2,1,0:T(8,128)S(1)}, u32[]{:S(2)}, u32[]{:S(2)}) collective-permute-start(f32[8,2,8,128]{3,2,1,0:T(8,128)S(1)} %get-tuple-element.27), channel_id=1, source_target_pairs={{0,4},{4,0},{8,12},{12,8},{16,20},{20,16},{24,28},{28,24},{32,36},... | collective-permute-start | bytes 196616 | tf_op jit(solution)/shard_map/ppermute | solution.py:326
  14.4 19.7 %collective-permute-start.5 = (f32[8,2,8,128]{3,2,1,0:T(8,128)S(1)}, f32[8,2,8,128]{3,2,1,0:T(8,128)S(1)}, u32[]{:S(2)}, u32[]{:S(2)}) collective-permute-start(f32[8,2,8,128]{3,2,1,0:T(8,128)S(1)} %get-tuple-element.25), channel_id=1, source_target_pairs={{0,0},{4,8},{8,4},{12,16},{16,12},{20,24},{24,20},{28,32},{32,28},... | collective-permute-start | bytes 196616 | tf_op jit(solution)/shard_map/ppermute | solution.py:327
  19.2 21.0 %all-to-all-start = ((f32[64,1,128]{2,1,0:T(1,128)}), f32[64,1,128]{2,1,0:T(1,128)S(1)}, u32[]{:S(2)}, u32[]{:S(2)}) async-start(f32[64,1,128]{2,1,0:T(1,128)} %add_wedges.1), calls=%async_computation | async-start | bytes 65536 | tf_op jit(solution)/shard_map/all_to_all | solution.py:303
